TPU v7x, 32 devices: a whole 2x2x4 slice. The times are simulated.
32 devices in a mesh: lat: 8 (over z, y), lon: 4 (over x, core).
Axes of the slice: x: 2, y: 2, z: 4, core: 2. Of those that a mesh axis runs over, the one named last changes fastest.
Arguments:
- features: bfloat16 [98304, 128], P(('lat', 'lon')), may hold values from -6 to 6
- cell_index: int32 [98304], P(('lat', 'lon')), may hold values from 0 to 2547
- tile_rows: int32 [1024], P(('lat', 'lon')), may hold values from 1 to 96, as said below
- spread: float32 [3, 3], replicated, may hold values from 0.2 to 1
- w_in: bfloat16 [128, 256], replicated, may hold values from -0.5 to 0.5
- w_dens: float32 [256], replicated, may hold values from -3 to 3
- w_one: bfloat16 [3, 3, 256, 256], replicated, may hold values from -0.125 to 0.125
- w_two: bfloat16 [3, 3, 256, 256], replicated, may hold values from -0.125 to 0.125
Outputs:
- encoded: bfloat16 [192, 384, 256], P('lat', 'lon')
Inputs may be any that keep to these rules, and one draw needn't show every extreme that they name: `tile_rows`: every block has 1 to 96 used slots; on every device some block has exactly 96.
All inputs are finite; a program needn't handle non-finite values.
Results may differ from a plain program's by a relative error of at most 0.0054.
Values may be sent and summed in bfloat16 or wider, within the bound.
A program may use at most 64 MiB of HBM per device.

v0:
```python
import functools

import jax
import jax.numpy as jnp
from jax import lax
from jax.experimental import pallas as pl
from jax.experimental.pallas import tpu as pltpu
from jax.sharding import PartitionSpec as P

TH = 24
TW = 96
F = 128
C = 256
CAP = 96
PH = 26
PW = 98
PWP = 112
GROUP = 8
HALF = PH // 2
ROWS = 12
MESH = pl.DeviceIdType.MESH
F32 = jnp.float32
BF16 = jnp.bfloat16


def xor(a, b, count):
    out = 0
    bit = 1
    while bit < count:
        out = out + ((a // bit + b // bit) % 2) * bit
        bit *= 2
    return out


def kernel(
    lat_n, lon_n,
    feats, raw, used, spread, w_in, w_dens, w_one, w_two, out,
    cells, out_v, rows_in, cells_in, lhs, acc, mean, logd, grid_x, hid_x, win_v, wone_v, wtwo_v,
    row_out, row_in, col_out, col_in, corner_in,
    row_send, row_recv, cell_send, cell_recv, own_sem, w_sem, out_sem, halo_send, halo_recv,
):
    n = lat_n * lon_n
    groups = n // GROUP
    lat = lax.axis_index("lat")
    lon = lax.axis_index("lon")
    me = lat * lon_n + lon
    my_group = me // GROUP
    my_place = me % GROUP
    east = (lon + 1) % lon_n
    west = (lon + lon_n - 1) % lon_n

    barrier = pltpu.get_barrier_semaphore()

    @pl.loop(1, n)
    def _(k):
        peer = (me + k) % n
        pl.semaphore_signal(
            barrier, inc=1, device_id=(peer // lon_n, peer % lon_n), device_id_type=MESH
        )

    lane = lax.broadcasted_iota(jnp.int32, (1, 128), 1)

    @pl.loop(0, n // 4)
    def _(quad):
        one, two, three = (raw[pl.ds(3 * quad + k, 1)] for k in range(3))
        picks = [
            one,
            jnp.where(lane < 32, pltpu.roll(one, 32, 1), pltpu.roll(two, 32, 1)),
            jnp.where(lane < 64, pltpu.roll(two, 64, 1), pltpu.roll(three, 64, 1)),
            pltpu.roll(three, 96, 1),
        ]
        for k, pick in enumerate(picks):
            row = ((pick.astype(F32) + 0.5) * (1.0 / PW)).astype(jnp.int32)
            code = row * 128 + (pick - row * PW)
            cells[4 * quad + k] = jnp.where(lane < used[4 * quad + k], code, 127 * 128)

    own = [
        pltpu.make_async_copy(feats.at[me], rows_in.at[me], own_sem.at[0]),
        pltpu.make_async_copy(cells.at[me], cells_in.at[me], own_sem.at[1]),
    ]
    weights = [
        pltpu.make_async_copy(w_in, win_v, w_sem.at[0]),
        pltpu.make_async_copy(w_one, wone_v, w_sem.at[1]),
        pltpu.make_async_copy(w_two, wtwo_v, w_sem.at[2]),
    ]
    for item in weights:
        item.start()
    pl.semaphore_wait(barrier, n - 1)

    def row_copy(src_block, slot, peer):
        return pltpu.make_async_remote_copy(
            src_ref=feats.at[src_block], dst_ref=rows_in.at[slot],
            send_sem=row_send.at[src_block], recv_sem=row_recv.at[slot],
            device_id=(peer // lon_n, peer % lon_n), device_id_type=MESH,
        )

    def cell_copy(src_block, slot, peer):
        return pltpu.make_async_remote_copy(
            src_ref=cells.at[src_block], dst_ref=cells_in.at[slot],
            send_sem=cell_send.at[src_block], recv_sem=cell_recv.at[slot],
            device_id=(peer // lon_n, peer % lon_n), device_id_type=MESH,
        )

    def peer_of(step):
        turn = 1 + step // GROUP
        return xor(my_group, turn, groups) * GROUP + (my_place + step % GROUP) % GROUP

    def each_peer(act):
        for place in range(1, GROUP):
            act(my_group * GROUP + (my_place + place) % GROUP)

        @pl.loop(0, n - GROUP)
        def _(step):
            act(peer_of(step))

    def send(peer):
        cell_copy(peer, me, peer).start()
        row_copy(peer, me, peer).start()

    each_peer(send)
    for item in own:
        item.start()

    acc[...] = jnp.zeros_like(acc)

    def add_group(base):
        enc = jnp.concatenate([cells_in[base + m][:, :CAP] for m in range(GROUP)], axis=1)
        wide = GROUP * CAP
        col = jnp.broadcast_to(enc & 127, (PWP, wide))
        col_hot = jnp.where(
            lax.broadcasted_iota(jnp.int32, (PWP, wide), 0) == col, 1.0, 0.0
        ).astype(BF16)
        row = jnp.broadcast_to(enc >> 7, (16, wide))
        rows = rows_in[pl.ds(base, GROUP)].reshape(wide, F)
        rhs = jnp.concatenate([rows, jnp.ones((wide, C - F), BF16)], axis=1)
        col_hot = col_hot.reshape(PWP // 16, 16, wide)
        for r in range(PH):
            here = jnp.where(row == r, 1.0, 0.0).astype(BF16)
            lhs[r] = (col_hot * here[None]).reshape(PWP, wide)
        for half in range(2):
            span = slice(half * HALF, (half + 1) * HALF)
            part = jnp.dot(
                lhs[span].reshape(HALF * PWP, wide), rhs, preferred_element_type=F32
            )
            acc[span] += part.reshape(HALF, PWP, C)

    for place in range(1, GROUP):
        peer = my_group * GROUP + (my_place + place) % GROUP
        cell_copy(peer, peer, peer).wait_recv()
        row_copy(peer, peer, peer).wait_recv()
    for item in own:
        item.wait()
    add_group(my_group * GROUP)

    @pl.loop(1, groups)
    def _(step):
        base = xor(my_group, step, groups) * GROUP
        for m in range(GROUP):
            cell_copy(base + m, base + m, base + m).wait_recv()
            row_copy(base + m, base + m, base + m).wait_recv()
        add_group(base)

    weights[0].wait()

    def put(x_ref, stage, r, value):
        x_ref[r + 1, :, C : 2 * C] = value.astype(BF16)
        x_ref[r + 1, :, 0:C] = pltpu.roll(value, 1, 0).astype(BF16)
        x_ref[r + 1, :, 2 * C :] = pltpu.roll(value, TW - 1, 0).astype(BF16)
        col_out[stage, 0, pl.ds(r, 1)] = value[0:1]
        col_out[stage, 1, pl.ds(r, 1)] = value[TW - 1 : TW]

    @pl.loop(0, TH, unroll=2)
    def _(r):
        parts = []
        for b in range(3):
            parts.append(
                sum(spread[a, b] * acc[r + a, 0:104] for a in range(3))
            )
        total = parts[0][0:TW] + parts[1][1 : TW + 1] + parts[2][2 : TW + 2]
        level = 1.0 + total[:, F:]
        mean[r] = (total[:, :F] / level).astype(BF16)
        logd[r] = jnp.log(level)

    @pl.loop(0, TH // ROWS)
    def _(step):
        start = step * ROWS
        grid = jnp.dot(
            mean[pl.ds(start, ROWS)].reshape(ROWS * TW, F), win_v[...],
            preferred_element_type=F32,
        ).reshape(ROWS, TW, C)
        for k in range(ROWS):
            lg = logd[start + k]
            value = grid[k] + jnp.concatenate([lg, lg], axis=1) * w_dens[...]
            put(grid_x, 0, start + k, value)

    def halo_copy(stage, kind, src, dst, where):
        return pltpu.make_async_remote_copy(
            src_ref=src, dst_ref=dst,
            send_sem=halo_send.at[stage, kind], recv_sem=halo_recv.at[stage, kind],
            device_id=where, device_id_type=MESH,
        )

    def copies(stage, x_ref):
        up, down = lat - 1, lat + 1
        left, right = col_out.at[stage, 0], col_out.at[stage, 1]
        both = [
            halo_copy(stage, 0, right, col_in.at[stage, 0], (lat, east)),
            halo_copy(stage, 1, left, col_in.at[stage, 1], (lat, west)),
        ]
        low, high = pl.ds(0, 8), pl.ds(TH - 8, 8)
        to_up = [
            halo_copy(stage, 2, row_out.at[stage, 0], row_in.at[stage, 1], (up, lon)),
            halo_copy(stage, 3, right.at[low], corner_in.at[stage, 2], (up, east)),
            halo_copy(stage, 4, left.at[low], corner_in.at[stage, 3], (up, west)),
        ]
        to_down = [
            halo_copy(stage, 5, row_out.at[stage, 1], row_in.at[stage, 0], (down, lon)),
            halo_copy(stage, 6, right.at[high], corner_in.at[stage, 0], (down, east)),
            halo_copy(stage, 7, left.at[high], corner_in.at[stage, 1], (down, west)),
        ]
        return both, to_up, to_down

    def set_edges(x_ref, r, left, right):
        ids = lax.broadcasted_iota(jnp.int32, (16, C), 0)
        first = x_ref[r, 0:16, 0:C].astype(F32)
        x_ref[r, 0:16, 0:C] = jnp.where(ids == 0, left, first).astype(BF16)
        last = x_ref[r, TW - 16 : TW, 2 * C :].astype(F32)
        x_ref[r, TW - 16 : TW, 2 * C :] = jnp.where(ids == 15, right, last).astype(BF16)

    def exchange(stage, x_ref, beside):
        row_out[stage, 0] = x_ref[1, :, C : 2 * C]
        row_out[stage, 1] = x_ref[TH, :, C : 2 * C]
        both, to_up, to_down = copies(stage, x_ref)
        for item in both:
            item.start()

        @pl.when(lat > 0)
        def _():
            for item in to_up:
                item.start()

        @pl.when(lat < lat_n - 1)
        def _():
            for item in to_down:
                item.start()

        beside()
        for item in both:
            item.wait_recv()

        for r in range(TH):
            set_edges(
                x_ref, r + 1, col_in[stage, 0, r : r + 1], col_in[stage, 1, r : r + 1]
            )

        def outer(r, side, corner_row):
            value = row_in[stage, side].astype(F32)
            x_ref[r, :, C : 2 * C] = row_in[stage, side]
            x_ref[r, :, 0:C] = pltpu.roll(value, 1, 0).astype(BF16)
            x_ref[r, :, 2 * C :] = pltpu.roll(value, TW - 1, 0).astype(BF16)
            rows = slice(corner_row, corner_row + 1)
            set_edges(
                x_ref, r, corner_in[stage, 2 * side, rows], corner_in[stage, 2 * side + 1, rows]
            )

        @pl.when(lat > 0)
        def _():
            for item in to_down:
                item.wait_recv()
            outer(0, 0, 7)

        @pl.when(lat == 0)
        def _():
            x_ref[0] = jnp.zeros((TW, 3 * C), BF16)

        @pl.when(lat < lat_n - 1)
        def _():
            for item in to_up:
                item.wait_recv()
            outer(TH + 1, 1, 0)

        @pl.when(lat == lat_n - 1)
        def _():
            x_ref[TH + 1] = jnp.zeros((TW, 3 * C), BF16)

    def drain(stage, x_ref):
        both, to_up, to_down = copies(stage, x_ref)
        for item in both:
            item.wait_send()

        @pl.when(lat > 0)
        def _():
            for item in to_up:
                item.wait_send()

        @pl.when(lat < lat_n - 1)
        def _():
            for item in to_down:
                item.wait_send()

    def conv(x_ref, weight, start):
        window = jnp.concatenate(
            [x_ref[pl.ds(start + a, ROWS)].reshape(ROWS * TW, 3 * C) for a in range(3)], axis=1
        )
        return jnp.dot(window, weight[...], preferred_element_type=F32).reshape(ROWS, TW, C)

    def sent(peer):
        cell_copy(peer, me, peer).wait_send()
        row_copy(peer, me, peer).wait_send()

    exchange(0, grid_x, lambda: each_peer(sent))
    weights[1].wait()

    @pl.loop(0, TH // ROWS)
    def _(step):
        start = step * ROWS
        total = conv(grid_x, wone_v, start)
        for k in range(ROWS):
            value = total[k]
            put(hid_x, 1, start + k, value / (1.0 + jnp.exp(-value)))

    exchange(1, hid_x, lambda: None)
    weights[2].wait()

    def out_copy(start):
        span = pl.ds(start, ROWS)
        return pltpu.make_async_copy(out_v.at[span], out.at[span], out_sem.at[start // ROWS])

    @pl.loop(0, TH // ROWS)
    def _(step):
        start = step * ROWS
        total = conv(hid_x, wtwo_v, start)
        base = grid_x[pl.ds(start + 1, ROWS), :, C : 2 * C].astype(F32)
        out_v[pl.ds(start, ROWS)] = (base + total).astype(BF16)
        out_copy(start).start()

    drain(0, grid_x)
    drain(1, hid_x)
    for step in range(TH // ROWS):
        out_copy(step * ROWS).wait()


def shards(features, cell_index, tile_rows, spread, w_in, w_dens, w_one, w_two):
    lat_n = lax.axis_size("lat")
    lon_n = lax.axis_size("lon")
    n = lat_n * lon_n
    hbm = pl.BlockSpec(memory_space=pltpu.HBM)
    anywhere = pl.BlockSpec(memory_space=pl.ANY)
    vmem = pl.BlockSpec(memory_space=pltpu.VMEM)
    smem = pl.BlockSpec(memory_space=pltpu.SMEM)
    dma = pltpu.SemaphoreType.DMA
    return pl.pallas_call(
        functools.partial(kernel, lat_n, lon_n),
        out_shape=jax.ShapeDtypeStruct((TH, TW, C), BF16),
        in_specs=[hbm, vmem, smem, smem, hbm, vmem, hbm, hbm],
        out_specs=anywhere,
        scratch_shapes=[
            pltpu.VMEM((n, 1, 128), jnp.int32),
            pltpu.VMEM((TH, TW, C), BF16),
            pltpu.VMEM((n, CAP, F), BF16),
            pltpu.VMEM((n, 1, 128), jnp.int32),
            pltpu.VMEM((PH, PWP, GROUP * CAP), BF16),
            pltpu.VMEM((PH, PWP, C), F32),
            pltpu.VMEM((TH, TW, F), BF16),
            pltpu.VMEM((TH, TW, F), F32),
            pltpu.VMEM((TH + 2, TW, 3 * C), BF16),
            pltpu.VMEM((TH + 2, TW, 3 * C), BF16),
            pltpu.VMEM((F, C), BF16),
            pltpu.VMEM((9 * C, C), BF16),
            pltpu.VMEM((9 * C, C), BF16),
            pltpu.VMEM((2, 2, TW, C), BF16),
            pltpu.VMEM((2, 2, TW, C), BF16),
            pltpu.VMEM((2, 2, TH, C), F32),
            pltpu.VMEM((2, 2, TH, C), F32),
            pltpu.VMEM((2, 4, 8, C), F32),
            dma((n,)), dma((n,)), dma((n,)), dma((n,)),
            dma((2,)), dma((3,)), dma((TH // ROWS,)), dma((2, 8)), dma((2, 8)),
        ],
        compiler_params=pltpu.CompilerParams(
            collective_id=0, has_side_effects=True, vmem_limit_bytes=60 * 1024 * 1024
        ),
    )(
        features.reshape(n, CAP, F), cell_index.reshape(-1, 128), tile_rows, spread, w_in, w_dens.reshape(1, C),
        w_one.reshape(9 * C, C), w_two.reshape(9 * C, C),
    )


def solution(mesh):
    blocks = P(("lat", "lon"))
    in_specs = (P(("lat", "lon"), None), blocks, blocks, P(), P(), P(), P(), P())
    out_specs = P("lat", "lon", None)
    return jax.shard_map(shards, mesh=mesh, in_specs=in_specs, out_specs=out_specs, check_vma=False)
```

profile of v0, /device:TPU:0, one launch (start us, length us, event | category | flops | bytes accessed | tf_op | source)
XLA Modules:
  0.0 50.4 jit_solution(15707316369228924881)
XLA Ops:
  0.0 48.1 %shard_map.82 = bf16[24,96,256]{2,1,0:T(8,128)(2,1)} custom-call(bf16[32,96,128]{2,1,0:T(8,128)(2,1)} %bitcast.7, s32[24,128]{1,0:T(8,128)} %bitcast.8, s32[32]{0:T(128)} %used.1, f32[3,3]{1,0:T(4,128)} %spread.1, bf16[128,256]{1,0:T(8,128)(2,1)} %w_in.1, f32[1,256]{1,0:T(1,128)} %bitcast.9, bf16[2304,256]{1,0:T(8,128)(2,1)} %bitcast.5, ...), custom_call_target="tpu_custom_call" | custom-call | tf_op jit(solution)/shard_map/pallas_call | solution.py:352
  48.1 2.4 %copy.10 = bf16[24,96,256]{2,1,0:T(8,128)(2,1)} copy(bf16[24,96,256]{2,1,0:T(8,128)(2,1)} %shard_map.82) | data formatting | bytes 2359296
where the time goes:
time: 50.6 us; the launch traced here: 50.4 us
  Pallas kernels  48.1 us (95%)
  local copies, waits for them, and re-layouts  2.36 us (5%)
    pallas_call x1, Pallas kernels, shards(): pl.pallas_call(functools.partial(kernel, lat_n, lon_n), out_shape=jax.Sha...  48.1 us
    unnamed x1, local copies, waits for them, and re-layouts  2.36 us

commit v1 on v0

v1 whole, which is shorter than its diff:
```python
import functools

import jax
import jax.numpy as jnp
from jax import lax
from jax.experimental import pallas as pl
from jax.experimental.pallas import tpu as pltpu
from jax.sharding import PartitionSpec as P

TH = 24
TW = 96
F = 128
C = 256
CAP = 96
PH = 26
PW = 98
GROUP = 8
WIDE = GROUP * CAP
PASS = 256
BLOCKS = WIDE // 128
SLOTS = 3
SIDE = 32
COLS = (0, 1, TW - 2, TW - 1)
MESH = pl.DeviceIdType.MESH
F32 = jnp.float32
BF16 = jnp.bfloat16


def kernel(
    lat_n, lon_n,
    feats, raw, used, spread, w_in, w_dens, w_one, w_two, out,
    cells, cells_in, rows_in, taps, hots, lhs0, lhs1, lhs2, lhs_col, acc, acc_col, acc_row, count, log_in, log_out,
    rhs_v, inv_b, log_b, grid_x, hid_x, mean_out, mean_in, col_out, col_in, corner_out, corner_in, sides, hid_side,
    out_v, win_v, wone_v, wtwo_v,
    row_send, row_recv, cell_send, cell_recv, own_sem, w_sem, out_sem, halo_send, halo_recv,
):
    lhs = (lhs0, lhs1, lhs2)
    n = lat_n * lon_n
    groups = n // GROUP
    lat = lax.axis_index("lat")
    lon = lax.axis_index("lon")
    me = lat * lon_n + lon
    east = (lon + 1) % lon_n
    west = (lon + lon_n - 1) % lon_n

    log_in[...] = jnp.zeros_like(log_in)
    bits = [1 << k for k in range(n.bit_length() - 1)]
    flips = [bit * (1 - 2 * (me // bit % 2)) for bit in bits]

    def across(d):
        return me + sum((d // bit % 2) * flip for bit, flip in zip(bits, flips))

    barrier = pltpu.get_barrier_semaphore()

    @pl.loop(1, n)
    def _(k):
        peer = (me + k) % n
        pl.semaphore_signal(
            barrier, inc=1, device_id=(peer // lon_n, peer % lon_n), device_id_type=MESH
        )

    weights = [
        pltpu.make_async_copy(w_in, win_v, w_sem.at[0]),
        pltpu.make_async_copy(w_one, wone_v, w_sem.at[1]),
        pltpu.make_async_copy(w_two, wtwo_v, w_sem.at[2]),
    ]
    for item in weights:
        item.start()

    lane = lax.broadcasted_iota(jnp.int32, (1, 128), 1)

    @pl.loop(0, n // 4)
    def _(quad):
        one, two, three = (raw[pl.ds(3 * quad + k, 1)] for k in range(3))
        picks = [
            one,
            jnp.where(lane < 32, pltpu.roll(one, 32, 1), pltpu.roll(two, 32, 1)),
            jnp.where(lane < 64, pltpu.roll(two, 64, 1), pltpu.roll(three, 64, 1)),
            pltpu.roll(three, 96, 1),
        ]
        for k, pick in enumerate(picks):
            row = ((pick.astype(F32) + 0.5) * (1.0 / PW)).astype(jnp.int32)
            code = row * 128 + (pick - row * PW)
            cells[4 * quad + k] = jnp.where(lane < used[4 * quad + k], code, 127 * 128)

    own = [
        pltpu.make_async_copy(feats.at[me], rows_in.at[0], own_sem.at[0]),
        pltpu.make_async_copy(cells.at[me], cells_in.at[0], own_sem.at[1]),
    ]
    count[...] = jnp.zeros_like(count)
    pl.semaphore_wait(barrier, n - 1)

    def cell_copy(d, peer):
        return pltpu.make_async_remote_copy(
            src_ref=cells.at[peer], dst_ref=cells_in.at[d],
            send_sem=cell_send.at[d], recv_sem=cell_recv.at[d],
            device_id=(peer // lon_n, peer % lon_n), device_id_type=MESH,
        )

    def row_copy(d, peer):
        return pltpu.make_async_remote_copy(
            src_ref=feats.at[peer], dst_ref=rows_in.at[d],
            send_sem=row_send.at[d], recv_sem=row_recv.at[d],
            device_id=(peer // lon_n, peer % lon_n), device_id_type=MESH,
        )

    for d in range(1, n):
        cell_copy(d, across(d)).start()
    for d in range(1, n):
        row_copy(d, across(d)).start()

    for item in own:
        item.start()

    def codes(group):
        enc = jnp.concatenate([cells_in[group * GROUP + m][:, :CAP] for m in range(GROUP)], axis=1)
        return enc & 127, enc >> 7

    def prepare(group, slot):
        col, row = codes(group)
        reach = jnp.broadcast_to(col, (TW, WIDE)) - lax.broadcasted_iota(jnp.int32, (TW, WIDE), 0)
        for a in range(3):
            tap = jnp.where(reach == 2, spread[a, 2], 0.0)
            tap = jnp.where(reach == 1, spread[a, 1], tap)
            taps[a] = jnp.where(reach == 0, spread[a, 0], tap).astype(BF16)
        wide_row = jnp.broadcast_to(row, (16, WIDE))
        for r in range(PH):
            hots[r] = jnp.where(wide_row == r, 1.0, 0.0).astype(BF16)
        above = jnp.broadcast_to(row, (SIDE, WIDE)) - lax.broadcasted_iota(jnp.int32, (SIDE, WIDE), 0)
        for k, c in enumerate(COLS):
            total = jnp.zeros((SIDE, WIDE), F32)
            for a in range(3):
                line = jnp.where(col == c + 2, spread[a, 2], 0.0)
                line = jnp.where(col == c + 1, spread[a, 1], line)
                line = jnp.where(col == c, spread[a, 0], line)
                total = jnp.where(above == a - 2, jnp.broadcast_to(line, (SIDE, WIDE)), total)
            lhs_col[slot, SIDE * k : SIDE * (k + 1)] = total.astype(BF16)

    def fill(block, slot):
        lanes = pl.ds(pl.multiple_of(block * 128, 128), 128)
        hot = [hots[r, :, lanes] for r in range(PH)]
        for strip in range(TW // 16):
            lines = slice(strip * 16, strip * 16 + 16)
            zero, one, two = (taps[a, lines, lanes] for a in range(3))
            for i in range(TH):
                lhs[slot][i, lines, lanes] = zero * hot[i] + one * hot[i + 1] + two * hot[i + 2]

    def build(group, slot):
        prepare(group, slot)

        @pl.loop(0, BLOCKS)
        def _(block):
            fill(block, slot)

    def cells_arrive(lo, hi):
        @pl.loop(lo, hi)
        def _(d):
            cell_copy(d, across(d)).wait_recv()

    own[1].wait()
    cells_arrive(1, GROUP)
    build(0, 0)
    if groups > 1:
        cells_arrive(GROUP, 2 * GROUP)
        build(1, 1)
    if groups > 2:
        cells_arrive(2 * GROUP, n)

    @pl.loop(0, groups)
    def _(group):
        col, row = codes(group)
        row_hot = jnp.where(
            lax.broadcasted_iota(jnp.int32, (SIDE, WIDE), 0) == row, 1.0, 0.0
        ).astype(BF16)
        col_hot = jnp.where(
            lax.broadcasted_iota(jnp.int32, (128, WIDE), 0) == col, 1.0, 0.0
        ).astype(BF16)
        count[...] += lax.dot_general(
            row_hot, col_hot, (((1,), (1,)), ((), ())), preferred_element_type=F32
        )

    density = jnp.zeros((SIDE, 128), F32)
    for a in range(3):
        line = count[...] if a == 2 else pltpu.roll(count[...], 2 - a, 0)
        for b in range(3):
            density += spread[a, b] * (line if b == 0 else pltpu.roll(line, 128 - b, 1))
    level = 1.0 + density
    inverse = 1.0 / level
    logs = jnp.log(level)
    log_out[0] = logs[0:8]
    log_out[1] = logs[SIDE - 8 : SIDE]

    def halo_copy(kind, src, dst, where):
        return pltpu.make_async_remote_copy(
            src_ref=src, dst_ref=dst, send_sem=halo_send.at[kind], recv_sem=halo_recv.at[kind],
            device_id=where, device_id_type=MESH,
        )

    up, down = lat - 1, lat + 1
    log_up = [halo_copy(0, log_out.at[0], log_in.at[1], (up, lon))]
    log_down = [halo_copy(1, log_out.at[1], log_in.at[0], (down, lon))]
    to_up = [
        halo_copy(2, mean_out.at[0], mean_in.at[1], (up, lon)),
        halo_copy(6, corner_out.at[0], corner_in.at[2], (up, east)),
        halo_copy(7, corner_out.at[1], corner_in.at[3], (up, west)),
    ]
    to_down = [
        halo_copy(3, mean_out.at[1], mean_in.at[0], (down, lon)),
        halo_copy(8, corner_out.at[2], corner_in.at[0], (down, east)),
        halo_copy(9, corner_out.at[3], corner_in.at[1], (down, west)),
    ]
    beside = [
        halo_copy(4, col_out.at[pl.ds(2, 2)], col_in.at[0], (lat, east)),
        halo_copy(5, col_out.at[pl.ds(0, 2)], col_in.at[1], (lat, west)),
    ]

    def when_up(act):
        @pl.when(lat > 0)
        def _():
            act()

    def when_down(act):
        @pl.when(lat < lat_n - 1)
        def _():
            act()

    def start_all(items):
        def act():
            for item in items:
                item.start()
        return act

    when_up(start_all(log_up))
    when_down(start_all(log_down))

    def features_of(group, lo, size):
        low, high = lo // CAP, -(-(lo + size) // CAP)
        rows = rows_in[pl.ds(group * GROUP + low, high - low)].reshape((high - low) * CAP, F)
        return rows[lo - low * CAP : lo - low * CAP + size]

    def add(group, slot, lo, size, first):
        rows = features_of(group, lo, size)
        span = slice(lo, lo + size)
        rhs = jnp.dot(rows, win_v[...], preferred_element_type=F32).astype(BF16)
        step = 12
        for i in range(0, TH, step):
            part = jnp.dot(
                lhs[slot][i : i + step, :, span].reshape(step * TW, size), rhs,
                preferred_element_type=F32,
            ).reshape(step, TW, C)
            acc[i : i + step] = part if first else acc[i : i + step] + part
        add_border(slot, rows, rhs, span, first)

    def add_beside(group, slot, later, spare, first):
        rows = features_of(group, 0, WIDE)
        rhs_v[...] = jnp.dot(rows, win_v[...], preferred_element_type=F32).astype(BF16)
        prepare(later, spare)
        size = TH // BLOCKS

        @pl.loop(0, BLOCKS)
        def _(block):
            lines = pl.ds(block * size, size)
            part = jnp.dot(
                lhs[slot][lines].reshape(size * TW, WIDE), rhs_v[...], preferred_element_type=F32
            ).reshape(size, TW, C)
            acc[lines] = part if first else acc[lines] + part
            fill(block, spare)

        add_border(slot, rows, rhs_v[...], slice(0, WIDE), first)

    def add_border(slot, rows, rhs, span, first):
        part = jnp.dot(lhs_col[slot, :, span], rhs, preferred_element_type=F32)
        acc_col[...] = part if first else acc_col[...] + part
        size = rows.shape[0]
        for k, i in ((0, 0), (2, TH - 2)):
            part = jnp.dot(
                lhs[slot][i : i + 2, :, span].reshape(2 * TW, size), rows,
                preferred_element_type=F32,
            ).reshape(2, TW, F)
            acc_row[k : k + 2] = part if first else acc_row[k : k + 2] + part

    def arrive(d):
        row_copy(d, across(d)).wait_recv()

    weights[0].wait()

    def wait_all(items):
        def act():
            for item in items:
                item.wait_recv()
        return act

    own[0].wait()
    if groups > 2:
        for d in range(1, GROUP):
            arrive(d)
        add_beside(0, 0, 2, 2, True)

    turned = jnp.transpose(jnp.concatenate([logs, jnp.zeros((128 - SIDE, 128), F32)], axis=0))
    for i in range(TH):
        log_b[i] = jnp.broadcast_to(turned[:TW, i + 2 : i + 3], (TW, 128))
    turned = jnp.transpose(
        jnp.concatenate([inverse, jnp.zeros((128 - SIDE, 128), F32)], axis=0)
    )
    for i in range(TH):
        inv_b[i] = jnp.broadcast_to(turned[:TW, i + 2 : i + 3], (TW, 128))

    for group in range(1, groups - 2):
        for m in range(GROUP):
            arrive(group * GROUP + m)
        add_beside(group, group % SLOTS, group + 2, (group + 2) % SLOTS, False)

    last = groups - 1
    slot = last % SLOTS
    for group in range(max(groups - 2, 0), groups):
        ready = 1 if group == 0 else 0
        for lo in range(0, WIDE - (PASS if group == last else 0), PASS):
            need = -(-(lo + PASS) // CAP)
            for m in range(ready, need):
                arrive(group * GROUP + m)
            ready = need
            add(group, group % SLOTS, lo, PASS, group == 0 and lo == 0)
    for m in range(ready, GROUP):
        arrive(last * GROUP + m)
    tail = slice(WIDE - PASS, WIDE)
    rows = features_of(last, WIDE - PASS, PASS)
    rhs = jnp.dot(rows, win_v[...], preferred_element_type=F32).astype(BF16)

    def scaled(total, t):
        factor, lg = inv_b[t - 2], log_b[t - 2]
        return total * jnp.concatenate([factor, factor], axis=1) + jnp.concatenate(
            [lg, lg], axis=1
        ) * w_dens[...]

    for k, i in ((0, 0), (2, TH - 2)):
        part = jnp.dot(
            lhs[slot][i : i + 2, :, tail].reshape(2 * TW, PASS), rows, preferred_element_type=F32
        ).reshape(2, TW, F)
        for m in range(2):
            mean_out[k // 2, m] = ((acc_row[k + m] + part[m]) * inv_b[i + m]).astype(BF16)
    when_up(to_up[0].start)
    when_down(to_down[0].start)
    part = acc_col[...] + jnp.dot(lhs_col[slot, :, tail], rhs, preferred_element_type=F32)
    inside = lax.broadcasted_iota(jnp.int32, (SIDE, C), 0)
    inside = (inside >= 2) & (inside < TH + 2)
    border = []
    for k, c in enumerate(COLS):
        factor = jnp.broadcast_to(inverse[:, c : c + 1], (SIDE, C))
        lg = jnp.broadcast_to(logs[:, c : c + 1], (SIDE, C))
        value = part[SIDE * k : SIDE * (k + 1)] * factor + lg * w_dens[...]
        value = jnp.where(inside, value, 0.0)
        border.append(value)
        col_out[k] = value.astype(BF16)
        sides[2 + k] = value
    for item in beside:
        item.start()
    pad = jnp.zeros((4, C), F32)
    for k, (line, pair) in enumerate(((2, 2), (2, 0), (TH, 2), (TH, 0))):
        corner_out[k] = jnp.concatenate(
            [border[pair][line : line + 2], border[pair + 1][line : line + 2], pad], axis=0
        )
    when_up(start_all(to_up[1:]))
    when_down(start_all(to_down[1:]))

    def put(x_ref, t, value):
        x_ref[t, :, C : 2 * C] = value.astype(BF16)
        x_ref[t, :, 0:C] = pltpu.roll(value, 1, 0).astype(BF16)
        x_ref[t, :, 2 * C :] = pltpu.roll(value, TW - 1, 0).astype(BF16)

    step = 6
    for i in range(0, TH, step):
        part = jnp.dot(
            lhs[slot][i : i + step, :, tail].reshape(step * TW, PASS), rhs,
            preferred_element_type=F32,
        ).reshape(step, TW, C)
        for k in range(step):
            put(grid_x, i + k + 2, scaled(acc[i + k] + part[k], i + k + 2))

    def conv(x_ref, weight, starts):
        window = jnp.concatenate(
            [
                jnp.concatenate([x_ref[s + a] for s in starts], axis=0)
                for a in range(3)
            ],
            axis=1,
        )
        return jnp.dot(window, weight[...], preferred_element_type=F32).reshape(len(starts), TW, C)

    def silu(value):
        return value / (1.0 + jnp.exp(-value))

    def hide(lines):
        total = conv(grid_x, wone_v, lines)
        for k, s in enumerate(lines):
            put(hid_x, s, silu(total[k]))

    def hide_sides():
        shifted = []
        for c in range(8):
            value = sides[c]
            shifted.append(
                [(value if a == 0 else pltpu.roll(value, SIDE - a, 0)).astype(BF16) for a in range(3)]
            )
        window = jnp.concatenate(
            [
                jnp.concatenate([shifted[c + b][a] for a in range(3) for b in range(3)], axis=1)
                for c in (0, 1, 4, 5)
            ],
            axis=0,
        )
        total = silu(jnp.dot(window, wone_v[...], preferred_element_type=F32))
        ids = lax.broadcasted_iota(jnp.int32, (SIDE, C), 0)
        keep = ((ids > 0) | (lat > 0)) & ((ids < TH + 1) | (lat < lat_n - 1))
        for k in range(4):
            hid_side[k] = jnp.where(keep, total[SIDE * k : SIDE * (k + 1)], 0.0)

    ids16 = lax.broadcasted_iota(jnp.int32, (16, C), 0)

    def patch(s):
        before, first, final, after = (hid_side[k, s : s + 1] for k in range(4))

        def edit(lines, lanes, picks):
            value = hid_x[s, lines, lanes].astype(F32)
            for at, line in picks:
                value = jnp.where(ids16 == at, line, value)
            hid_x[s, lines, lanes] = value.astype(BF16)

        low, high = slice(0, 16), slice(TW - 16, TW)
        edit(low, slice(0, C), ((0, before), (1, first)))
        edit(low, slice(C, 2 * C), ((0, first),))
        edit(high, slice(C, 2 * C), ((15, final),))
        edit(high, slice(2 * C, 3 * C), ((14, final), (15, after)))

    def out_copy(lo, size):
        span = pl.ds(lo, size)
        return pltpu.make_async_copy(out_v.at[span], out.at[span], out_sem.at[lo])

    def encode(lines):
        total = conv(hid_x, wtwo_v, lines)
        for k, o in enumerate(lines):
            out_v[o] = (grid_x[o + 2, :, C : 2 * C].astype(F32) + total[k]).astype(BF16)

    weights[1].wait()
    for s in range(2, TH, 2):
        hide((s, s + 1))

    for item in beside:
        item.wait_recv()
    for k in range(2):
        sides[k] = col_in[0, k].astype(F32)
        sides[6 + k] = col_in[1, k].astype(F32)
    hide_sides()
    for s in range(2, TH):
        patch(s)
    weights[2].wait()
    for o in range(2, TH - 2, 2):
        encode((o, o + 1))
    out_copy(2, TH - 4).start()

    def outer(side):
        base = (0, TH + 2)[side]
        value = jnp.dot(
            mean_in[side].reshape(2 * TW, F), win_v[...], preferred_element_type=F32
        ).reshape(2, TW, C)
        turned = jnp.transpose(jnp.concatenate([log_in[side], jnp.zeros((120, 128), F32)], axis=0))
        for m in range(2):
            at = m if side == 0 else m + 2
            lg = jnp.broadcast_to(turned[:TW, at : at + 1], (TW, 128))
            line = value[m] + jnp.concatenate([lg, lg], axis=1) * w_dens[...]
            put(grid_x, base + m, line)
            for k, c in enumerate(COLS):
                sides[2 + k, base + m : base + m + 1] = line[c : c + 1]
        for k, c in enumerate((0, 1, 6, 7)):
            pair, line = k // 2, k % 2
            sides[c, base : base + 2] = corner_in[2 * side + pair, 2 * line : 2 * line + 2]

    def above():
        wait_all(log_down + to_down)()
        outer(0)

    def below():
        wait_all(log_up + to_up)()
        outer(1)

    when_up(above)
    when_down(below)

    @pl.when(lat == 0)
    def _():
        grid_x[0:2] = jnp.zeros((2, TW, 3 * C), BF16)

    @pl.when(lat == lat_n - 1)
    def _():
        grid_x[TH + 2 : TH + 4] = jnp.zeros((2, TW, 3 * C), BF16)

    hide((0, 1, TH, TH + 1))
    hide_sides()
    for s in (0, 1, TH, TH + 1):
        patch(s)

    @pl.when(lat == 0)
    def _():
        hid_x[0] = jnp.zeros((TW, 3 * C), BF16)

    @pl.when(lat == lat_n - 1)
    def _():
        hid_x[TH + 1] = jnp.zeros((TW, 3 * C), BF16)

    encode((0, 1, TH - 2, TH - 1))
    out_copy(0, 2).start()
    out_copy(TH - 2, 2).start()

    @pl.loop(1, n)
    def _(d):
        peer = across(d)
        cell_copy(d, peer).wait_send()
        row_copy(d, peer).wait_send()

    def drain(items):
        def act():
            for item in items:
                item.wait_send()
        return act

    drain(beside)()
    when_up(drain(log_up + to_up))
    when_down(drain(log_down + to_down))
    out_copy(2, TH - 4).wait()
    out_copy(0, 2).wait()
    out_copy(TH - 2, 2).wait()


def shards(features, cell_index, tile_rows, spread, w_in, w_dens, w_one, w_two):
    lat_n = lax.axis_size("lat")
    lon_n = lax.axis_size("lon")
    n = lat_n * lon_n
    hbm = pl.BlockSpec(memory_space=pltpu.HBM)
    anywhere = pl.BlockSpec(memory_space=pl.ANY)
    vmem = pl.BlockSpec(memory_space=pltpu.VMEM)
    smem = pl.BlockSpec(memory_space=pltpu.SMEM)
    dma = pltpu.SemaphoreType.DMA
    return pl.pallas_call(
        functools.partial(kernel, lat_n, lon_n),
        out_shape=jax.ShapeDtypeStruct((TH, TW, C), BF16),
        in_specs=[hbm, vmem, smem, smem, hbm, vmem, hbm, hbm],
        out_specs=anywhere,
        scratch_shapes=[
            pltpu.VMEM((n, 1, 128), jnp.int32),
            pltpu.VMEM((n, 1, 128), jnp.int32),
            pltpu.VMEM((n, CAP, F), BF16),
            pltpu.VMEM((3, TW, WIDE), BF16),
            pltpu.VMEM((PH, 16, WIDE), BF16),
            pltpu.VMEM((TH, TW, WIDE), BF16),
            pltpu.VMEM((TH, TW, WIDE), BF16),
            pltpu.VMEM((TH, TW, WIDE), BF16),
            pltpu.VMEM((SLOTS, 4 * SIDE, WIDE), BF16),
            pltpu.VMEM((TH, TW, C), F32),
            pltpu.VMEM((4 * SIDE, C), F32),
            pltpu.VMEM((4, TW, F), F32),
            pltpu.VMEM((SIDE, 128), F32),
            pltpu.VMEM((2, 8, 128), F32),
            pltpu.VMEM((2, 8, 128), F32),
            pltpu.VMEM((WIDE, C), BF16),
            pltpu.VMEM((TH, TW, 128), F32),
            pltpu.VMEM((TH, TW, 128), F32),
            pltpu.VMEM((TH + 4, TW, 3 * C), BF16),
            pltpu.VMEM((TH + 2, TW, 3 * C), BF16),
            pltpu.VMEM((2, 2, TW, F), BF16),
            pltpu.VMEM((2, 2, TW, F), BF16),
            pltpu.VMEM((4, SIDE, C), BF16),
            pltpu.VMEM((2, 2, SIDE, C), BF16),
            pltpu.VMEM((4, 8, C), F32),
            pltpu.VMEM((4, 8, C), F32),
            pltpu.VMEM((8, SIDE, C), F32),
            pltpu.VMEM((4, SIDE, C), F32),
            pltpu.VMEM((TH, TW, C), BF16),
            pltpu.VMEM((F, C), BF16),
            pltpu.VMEM((9 * C, C), BF16),
            pltpu.VMEM((9 * C, C), BF16),
            dma((n,)), dma((n,)), dma((n,)), dma((n,)),
            dma((2,)), dma((3,)), dma((TH,)), dma((10,)), dma((10,)),
        ],
        compiler_params=pltpu.CompilerParams(
            collective_id=0, has_side_effects=True, vmem_limit_bytes=60 * 1024 * 1024
        ),
    )(
        features.reshape(n, CAP, F), cell_index.reshape(-1, 128), tile_rows, spread, w_in, w_dens.reshape(1, C),
        w_one.reshape(9 * C, C), w_two.reshape(9 * C, C),
    )


def solution(mesh):
    blocks = P(("lat", "lon"))
    in_specs = (P(("lat", "lon"), None), blocks, blocks, P(), P(), P(), P(), P())
    out_specs = P("lat", "lon", None)
    return jax.shard_map(shards, mesh=mesh, in_specs=in_specs, out_specs=out_specs, check_vma=False)
```

time: 50.6 us -> 41.8 us (0.83)
  Pallas kernels: 48.1 us -> 39.2 us
    pallas_call x1, Pallas kernels: 48.1 us -> 39.2 us  [shards(): pl.pallas_call(functools.partial(kernel, lat_n, lon_n), out_shape=jax.Sha...]
where the time goes in v1:
time: 41.8 us; the launch traced here: 41.6 us
  Pallas kernels  39.2 us (94%)
  local copies, waits for them, and re-layouts  2.36 us (6%)
    pallas_call x1, Pallas kernels, shards(): pl.pallas_call(functools.partial(kernel, lat_n, lon_n), out_shape=jax.Sha...  39.2 us
    unnamed x1, local copies, waits for them, and re-layouts  2.36 us

profile of v1, /device:TPU:0, one launch (start us, length us, event | category | flops | bytes accessed | tf_op | source)
XLA Modules:
  0.0 41.6 jit_solution(13037927819306760320)
XLA Ops:
  0.0 39.2 %shard_map.82 = bf16[24,96,256]{2,1,0:T(8,128)(2,1)} custom-call(bf16[32,96,128]{2,1,0:T(8,128)(2,1)} %bitcast.7, s32[24,128]{1,0:T(8,128)} %bitcast.8, s32[32]{0:T(128)} %used.1, f32[3,3]{1,0:T(4,128)} %spread.1, bf16[128,256]{1,0:T(8,128)(2,1)} %w_in.1, f32[1,256]{1,0:T(1,128)} %bitcast.9, bf16[2304,256]{1,0:T(8,128)(2,1)} %bitcast.5, ...), custom_call_target="tpu_custom_call" | custom-call | tf_op jit(solution)/shard_map/pallas_call | solution.py:542
  39.2 2.4 %copy.10 = bf16[24,96,256]{2,1,0:T(8,128)(2,1)} copy(bf16[24,96,256]{2,1,0:T(8,128)(2,1)} %shard_map.82) | data formatting | bytes 2359296

commit v2 on v1

--- a/solution.py
+++ b/solution.py
@@ -18,7 +18,9 @@
 WIDE = GROUP * CAP
 PASS = 256
 BLOCKS = WIDE // 128
-SLOTS = 3
+SLOTS = 4
+VMEM = 67043328
+HELD = 2 * C * (TH * TW + (TH + 4) * TW + 3 * (TH + 2) * TW + 9 * C)
 SIDE = 32
 COLS = (0, 1, TW - 2, TW - 1)
 MESH = pl.DeviceIdType.MESH
@@ -26,15 +28,26 @@
 BF16 = jnp.bfloat16
 
 
+def conv(x_ref, weight, starts):
+    window = jnp.concatenate(
+        [
+            jnp.concatenate([x_ref[s + a] for s in starts], axis=0)
+            for a in range(3)
+        ],
+        axis=1,
+    )
+    return jnp.dot(window, weight[...], preferred_element_type=F32).reshape(len(starts), TW, C)
+
+
 def kernel(
     lat_n, lon_n,
-    feats, raw, used, spread, w_in, w_dens, w_one, w_two, out,
-    cells, cells_in, rows_in, taps, hots, lhs0, lhs1, lhs2, lhs_col, acc, acc_col, acc_row, count, log_in, log_out,
-    rhs_v, inv_b, log_b, grid_x, hid_x, mean_out, mean_in, col_out, col_in, corner_out, corner_in, sides, hid_side,
-    out_v, win_v, wone_v, wtwo_v,
-    row_send, row_recv, cell_send, cell_recv, own_sem, w_sem, out_sem, halo_send, halo_recv,
+    feats, raw, used, spread, w_in, w_dens, w_one, w_two, out_v, grid_x, hid_x, wtwo_v,
+    cells, cells_in, rows_in, taps, hots, lhs0, lhs1, lhs2, lhs3, lhs_col, acc, acc_col, acc_row, count, log_in, log_out,
+    rhs_v, inv_b, log_b, mean_out, mean_in, col_out, col_in, corner_out, corner_in, sides, hid_side,
+    win_v, wone_v,
+    row_send, row_recv, cell_send, cell_recv, own_sem, w_sem, halo_send, halo_recv,
 ):
-    lhs = (lhs0, lhs1, lhs2)
+    lhs = (lhs0, lhs1, lhs2, lhs3)
     n = lat_n * lon_n
     groups = n // GROUP
     lat = lax.axis_index("lat")
@@ -305,10 +318,16 @@
     for i in range(TH):
         inv_b[i] = jnp.broadcast_to(turned[:TW, i + 2 : i + 3], (TW, 128))
 
+    if groups > 3:
+        build(3, 3)
     for group in range(1, groups - 2):
         for m in range(GROUP):
             arrive(group * GROUP + m)
-        add_beside(group, group % SLOTS, group + 2, (group + 2) % SLOTS, False)
+        later = group + 3
+        if later < groups:
+            add_beside(group, group % SLOTS, later, later % SLOTS, False)
+        else:
+            add(group, group % SLOTS, 0, WIDE, False)
 
     last = groups - 1
     slot = last % SLOTS
@@ -374,25 +393,26 @@
             preferred_element_type=F32,
         ).reshape(step, TW, C)
         for k in range(step):
-            put(grid_x, i + k + 2, scaled(acc[i + k] + part[k], i + k + 2))
-
-    def conv(x_ref, weight, starts):
-        window = jnp.concatenate(
-            [
-                jnp.concatenate([x_ref[s + a] for s in starts], axis=0)
-                for a in range(3)
-            ],
-            axis=1,
-        )
-        return jnp.dot(window, weight[...], preferred_element_type=F32).reshape(len(starts), TW, C)
+            grid_x[i + k + 2] = scaled(acc[i + k] + part[k], i + k + 2).astype(BF16)
 
     def silu(value):
         return value / (1.0 + jnp.exp(-value))
 
     def hide(lines):
-        total = conv(grid_x, wone_v, lines)
+        window = jnp.concatenate(
+            [jnp.concatenate([grid_x[s + a] for s in lines], axis=0) for a in range(3)], axis=1
+        )
+        left, middle, right = (
+            jnp.dot(
+                window,
+                jnp.concatenate([wone_v[(3 * a + b) * C : (3 * a + b + 1) * C] for a in range(3)], axis=0),
+                preferred_element_type=F32,
+            ).reshape(len(lines), TW, C)
+            for b in range(3)
+        )
         for k, s in enumerate(lines):
-            put(hid_x, s, silu(total[k]))
+            total = pltpu.roll(left[k], 1, 0) + middle[k] + pltpu.roll(right[k], TW - 1, 0)
+            put(hid_x, s, silu(total))
 
     def hide_sides():
         shifted = []
@@ -431,14 +451,10 @@
         edit(high, slice(C, 2 * C), ((15, final),))
         edit(high, slice(2 * C, 3 * C), ((14, final), (15, after)))
 
-    def out_copy(lo, size):
-        span = pl.ds(lo, size)
-        return pltpu.make_async_copy(out_v.at[span], out.at[span], out_sem.at[lo])
-
     def encode(lines):
         total = conv(hid_x, wtwo_v, lines)
         for k, o in enumerate(lines):
-            out_v[o] = (grid_x[o + 2, :, C : 2 * C].astype(F32) + total[k]).astype(BF16)
+            out_v[o] = (grid_x[o + 2].astype(F32) + total[k]).astype(BF16)
 
     weights[1].wait()
     for s in range(2, TH, 2):
@@ -455,7 +471,6 @@
     weights[2].wait()
     for o in range(2, TH - 2, 2):
         encode((o, o + 1))
-    out_copy(2, TH - 4).start()
 
     def outer(side):
         base = (0, TH + 2)[side]
@@ -467,7 +482,7 @@
             at = m if side == 0 else m + 2
             lg = jnp.broadcast_to(turned[:TW, at : at + 1], (TW, 128))
             line = value[m] + jnp.concatenate([lg, lg], axis=1) * w_dens[...]
-            put(grid_x, base + m, line)
+            grid_x[base + m] = line.astype(BF16)
             for k, c in enumerate(COLS):
                 sides[2 + k, base + m : base + m + 1] = line[c : c + 1]
         for k, c in enumerate((0, 1, 6, 7)):
@@ -487,11 +502,11 @@
 
     @pl.when(lat == 0)
     def _():
-        grid_x[0:2] = jnp.zeros((2, TW, 3 * C), BF16)
+        grid_x[0:2] = jnp.zeros((2, TW, C), BF16)
 
     @pl.when(lat == lat_n - 1)
     def _():
-        grid_x[TH + 2 : TH + 4] = jnp.zeros((2, TW, 3 * C), BF16)
+        grid_x[TH + 2 : TH + 4] = jnp.zeros((2, TW, C), BF16)
 
     hide((0, 1, TH, TH + 1))
     hide_sides()
@@ -505,10 +520,6 @@
     @pl.when(lat == lat_n - 1)
     def _():
         hid_x[TH + 1] = jnp.zeros((TW, 3 * C), BF16)
-
-    encode((0, 1, TH - 2, TH - 1))
-    out_copy(0, 2).start()
-    out_copy(TH - 2, 2).start()
 
     @pl.loop(1, n)
     def _(d):
@@ -525,9 +536,26 @@
     drain(beside)()
     when_up(drain(log_up + to_up))
     when_down(drain(log_down + to_down))
-    out_copy(2, TH - 4).wait()
-    out_copy(0, 2).wait()
-    out_copy(TH - 2, 2).wait()
+
+
+def finish(inner, grid_x, hid_x, weight, out, outer, sem):
+    def copy(src, lo, size, k):
+        return pltpu.make_async_copy(src, out.at[pl.ds(lo, size)], sem.at[k])
+
+    copies = [
+        copy(inner.at[pl.ds(2, TH - 4)], 2, TH - 4, 0),
+        copy(outer.at[pl.ds(0, 2)], 0, 2, 1),
+        copy(outer.at[pl.ds(2, 2)], TH - 2, 2, 2),
+    ]
+    copies[0].start()
+    lines = (0, 1, TH - 2, TH - 1)
+    total = conv(hid_x, weight, lines)
+    for k, o in enumerate(lines):
+        outer[k] = (grid_x[o + 2].astype(F32) + total[k]).astype(BF16)
+    for item in copies[1:]:
+        item.start()
+    for item in copies:
+        item.wait()
 
 
 def shards(features, cell_index, tile_rows, spread, w_in, w_dens, w_one, w_two):
@@ -539,17 +567,23 @@
     vmem = pl.BlockSpec(memory_space=pltpu.VMEM)
     smem = pl.BlockSpec(memory_space=pltpu.SMEM)
     dma = pltpu.SemaphoreType.DMA
-    return pl.pallas_call(
+    held = pl.pallas_call(
         functools.partial(kernel, lat_n, lon_n),
-        out_shape=jax.ShapeDtypeStruct((TH, TW, C), BF16),
+        out_shape=[
+            pltpu.VMEM((TH, TW, C), BF16),
+            pltpu.VMEM((TH + 4, TW, C), BF16),
+            pltpu.VMEM((TH + 2, TW, 3 * C), BF16),
+            pltpu.VMEM((9 * C, C), BF16),
+        ],
         in_specs=[hbm, vmem, smem, smem, hbm, vmem, hbm, hbm],
-        out_specs=anywhere,
+        out_specs=[vmem] * 4,
         scratch_shapes=[
             pltpu.VMEM((n, 1, 128), jnp.int32),
             pltpu.VMEM((n, 1, 128), jnp.int32),
             pltpu.VMEM((n, CAP, F), BF16),
             pltpu.VMEM((3, TW, WIDE), BF16),
             pltpu.VMEM((PH, 16, WIDE), BF16),
+            pltpu.VMEM((TH, TW, WIDE), BF16),
             pltpu.VMEM((TH, TW, WIDE), BF16),
             pltpu.VMEM((TH, TW, WIDE), BF16),
             pltpu.VMEM((TH, TW, WIDE), BF16),
@@ -563,8 +597,6 @@
             pltpu.VMEM((WIDE, C), BF16),
             pltpu.VMEM((TH, TW, 128), F32),
             pltpu.VMEM((TH, TW, 128), F32),
-            pltpu.VMEM((TH + 4, TW, 3 * C), BF16),
-            pltpu.VMEM((TH + 2, TW, 3 * C), BF16),
             pltpu.VMEM((2, 2, TW, F), BF16),
             pltpu.VMEM((2, 2, TW, F), BF16),
             pltpu.VMEM((4, SIDE, C), BF16),
@@ -573,20 +605,26 @@
             pltpu.VMEM((4, 8, C), F32),
             pltpu.VMEM((8, SIDE, C), F32),
             pltpu.VMEM((4, SIDE, C), F32),
-            pltpu.VMEM((TH, TW, C), BF16),
             pltpu.VMEM((F, C), BF16),
             pltpu.VMEM((9 * C, C), BF16),
-            pltpu.VMEM((9 * C, C), BF16),
             dma((n,)), dma((n,)), dma((n,)), dma((n,)),
-            dma((2,)), dma((3,)), dma((TH,)), dma((10,)), dma((10,)),
+            dma((2,)), dma((3,)), dma((10,)), dma((10,)),
         ],
         compiler_params=pltpu.CompilerParams(
-            collective_id=0, has_side_effects=True, vmem_limit_bytes=60 * 1024 * 1024
+            collective_id=0, has_side_effects=True, vmem_limit_bytes=VMEM - HELD
         ),
     )(
         features.reshape(n, CAP, F), cell_index.reshape(-1, 128), tile_rows, spread, w_in, w_dens.reshape(1, C),
         w_one.reshape(9 * C, C), w_two.reshape(9 * C, C),
     )
+    return pl.pallas_call(
+        finish,
+        out_shape=jax.ShapeDtypeStruct((TH, TW, C), BF16),
+        in_specs=[vmem] * 4,
+        out_specs=anywhere,
+        scratch_shapes=[pltpu.VMEM((4, TW, C), BF16), dma((3,))],
+        compiler_params=pltpu.CompilerParams(vmem_limit_bytes=16 * 1024 * 1024),
+    )(*held)
 
 
 def solution(mesh):

time: 41.8 us -> 37.6 us (0.90)
  local copies, waits for them, and re-layouts: 2.36 us -> 0 us
  Pallas kernels: 39.2 us -> 37.2 us
    unnamed x1 -> x0, local copies, waits for them, and re-layouts: 2.36 us -> none
    pallas_call x1 -> x2, Pallas kernels: 39.2 us -> 37.2 us  [the longest x1 35.9 us: shards(): pl.pallas_call(functools.partial(kernel, lat_n, lon_n), out_shape=[pltpu....]
where the time goes in v2:
time: 37.6 us; the launch traced here: 37.4 us
  Pallas kernels  37.2 us (99%)
    pallas_call x1, Pallas kernels, shards(): pl.pallas_call(functools.partial(kernel, lat_n, lon_n), out_shape=[pltpu....  35.9 us
    pallas_call x1, Pallas kernels, shards(): pl.pallas_call(finish, out_shape=jax.ShapeDtypeStruct((TH, TW, C), BF16),...  1.33 us

profile of v2, /device:TPU:0, one launch (start us, length us, event | category | flops | bytes accessed | tf_op | source)
XLA Modules:
  0.0 37.4 jit_solution(959029495824128342)
XLA Ops:
  0.0 35.9 %shard_map.82 = (bf16[24,96,256]{2,1,0:T(8,128)(2,1)S(1)}, bf16[28,96,256]{2,1,0:T(8,128)(2,1)S(1)}, bf16[26,96,768]{2,1,0:T(8,128)(2,1)S(1)}, bf16[2304,256]{1,0:T(8,128)(2,1)S(1)}) custom-call(bf16[32,96,128]{2,1,0:T(8,128)(2,1)} %bitcast.7, s32[24,128]{1,0:T(8,128)} %bitcast.8, s32[32]{0:T(128)} %used.1, f32[3,3]{1,0:T(4,128)} %spread.1, ...), custom_call_target="tpu_custom_call" | custom-call | tf_op jit(solution)/shard_map/pallas_call | solution.py:570
  35.9 1.3 %shard_map.83 = bf16[24,96,256]{2,1,0:T(8,128)(2,1)} custom-call(bf16[24,96,256]{2,1,0:T(8,128)(2,1)S(1)} %get-tuple-element.9.inner, bf16[28,96,256]{2,1,0:T(8,128)(2,1)S(1)} %get-tuple-element.10.grid_x, bf16[26,96,768]{2,1,0:T(8,128)(2,1)S(1)} %get-tuple-element.11.hid_x, bf16[2304,256]{1,0:T(8,128)(2,1)S(1)} %get-tuple-element.12.weight), custom_call_target="tpu_custom_call" | custom-call | tf_op jit(solution)/shard_map/pallas_call | solution.py:620

commit v3 on v2

--- a/solution.py
+++ b/solution.py
@@ -16,7 +16,7 @@
 PW = 98
 GROUP = 8
 WIDE = GROUP * CAP
-PASS = 256
+PASS = WIDE // 2
 BLOCKS = WIDE // 128
 SLOTS = 4
 VMEM = 67043328
@@ -166,8 +166,7 @@
             fill(block, slot)
 
     def cells_arrive(lo, hi):
-        @pl.loop(lo, hi)
-        def _(d):
+        for d in range(lo, hi):
             cell_copy(d, across(d)).wait_recv()
 
     own[1].wait()
@@ -305,9 +304,13 @@
 
     own[0].wait()
     if groups > 2:
+        build(2, 2)
         for d in range(1, GROUP):
             arrive(d)
-        add_beside(0, 0, 2, 2, True)
+        if groups > 3:
+            add_beside(0, 0, 3, 3, True)
+        else:
+            add(0, 0, 0, WIDE, True)
 
     turned = jnp.transpose(jnp.concatenate([logs, jnp.zeros((128 - SIDE, 128), F32)], axis=0))
     for i in range(TH):
@@ -318,8 +321,6 @@
     for i in range(TH):
         inv_b[i] = jnp.broadcast_to(turned[:TW, i + 2 : i + 3], (TW, 128))
 
-    if groups > 3:
-        build(3, 3)
     for group in range(1, groups - 2):
         for m in range(GROUP):
             arrive(group * GROUP + m)
@@ -472,6 +473,10 @@
     for o in range(2, TH - 2, 2):
         encode((o, o + 1))
 
+    for d in range(1, n):
+        cell_copy(d, across(d)).wait_send()
+        row_copy(d, across(d)).wait_send()
+
     def outer(side):
         base = (0, TH + 2)[side]
         value = jnp.dot(
@@ -520,12 +525,6 @@
     @pl.when(lat == lat_n - 1)
     def _():
         hid_x[TH + 1] = jnp.zeros((TW, 3 * C), BF16)
-
-    @pl.loop(1, n)
-    def _(d):
-        peer = across(d)
-        cell_copy(d, peer).wait_send()
-        row_copy(d, peer).wait_send()
 
     def drain(items):
         def act():

time: 37.6 us -> 37.3 us (level)
  no operation moved by 1% of the time
where the time goes in v3:
time: 37.3 us; the launch traced here: 37.1 us
  Pallas kernels  37 us (99%)
    pallas_call x1, Pallas kernels, shards(): pl.pallas_call(functools.partial(kernel, lat_n, lon_n), out_shape=[pltpu....  35.6 us
    pallas_call x1, Pallas kernels, shards(): pl.pallas_call(finish, out_shape=jax.ShapeDtypeStruct((TH, TW, C), BF16),...  1.33 us

profile of v3, /device:TPU:0, one launch (start us, length us, event | category | flops | bytes accessed | tf_op | source)
XLA Modules:
  0.0 37.1 jit_solution(16285270668527324606)
XLA Ops:
  0.0 35.6 %shard_map.82 = (bf16[24,96,256]{2,1,0:T(8,128)(2,1)S(1)}, bf16[28,96,256]{2,1,0:T(8,128)(2,1)S(1)}, bf16[26,96,768]{2,1,0:T(8,128)(2,1)S(1)}, bf16[2304,256]{1,0:T(8,128)(2,1)S(1)}) custom-call(bf16[32,96,128]{2,1,0:T(8,128)(2,1)} %bitcast.7, s32[24,128]{1,0:T(8,128)} %bitcast.8, s32[32]{0:T(128)} %used.1, f32[3,3]{1,0:T(4,128)} %spread.1, ...), custom_call_target="tpu_custom_call" | custom-call | tf_op jit(solution)/shard_map/pallas_call | solution.py:569
  35.6 1.3 %shard_map.83 = bf16[24,96,256]{2,1,0:T(8,128)(2,1)} custom-call(bf16[24,96,256]{2,1,0:T(8,128)(2,1)S(1)} %get-tuple-element.9.inner, bf16[28,96,256]{2,1,0:T(8,128)(2,1)S(1)} %get-tuple-element.10.grid_x, bf16[26,96,768]{2,1,0:T(8,128)(2,1)S(1)} %get-tuple-element.11.hid_x, bf16[2304,256]{1,0:T(8,128)(2,1)S(1)} %get-tuple-element.12.weight), custom_call_target="tpu_custom_call" | custom-call | tf_op jit(solution)/shard_map/pallas_call | solution.py:619
